TPU v7x, 32 devices: a whole 2x2x4 slice. The times are simulated.
32 devices in a mesh: samp: 16 (over z, y, x), feat: 2 (over core).
Axes of the slice: x: 2, y: 2, z: 4, core: 2. Of those that a mesh axis runs over, the one named last changes fastest.
Arguments:
- design_matrix: bfloat16 [2048, 32768], P('samp', 'feat'), may hold values from -0.046875 to 0.046875
- labels: int32 [2048], P('samp'), may hold values from 0 to 1
- weights: float32 [16, 32768], P(None, ('feat', 'samp')), may hold values from -6 to 6
- lambdas: float32 [16], replicated, may hold values from 0.05 to 1
- sketch: bfloat16 [32768, 384], P(('feat', 'samp')), may hold values from -0.03125 to 0.03125
- sketch_values: float32 [384], replicated, may hold values from 0.05 to 2
Outputs:
- new_weights: float32 [16, 32768], P(None, ('feat', 'samp'))
All inputs are finite; a program needn't handle non-finite values.
Results may differ from a plain program's by a relative error of at most 0.004.
Values may be sent and summed in bfloat16 or wider, within the bound.
No kernel may reach another device: no remote copies, remote signals or barrier semaphores. Data moves between devices by JAX's collectives and lax.ppermute only.
A program may use at most 64 MiB of HBM per device.

v0:
```python
import jax
import jax.numpy as jnp
from jax import lax
from jax.sharding import PartitionSpec as P

ITERS = 2


def shards(design_matrix, labels, weights, lambdas, sketch, sketch_values):
    sketch_full = sketch.astype(jnp.float32)
    smallest = jnp.min(sketch_values)
    ratios = (smallest + lambdas[:, None]) / (sketch_values[None, :] + lambdas[:, None]) - 1.0

    def apply_rows(vector):
        vector_half = vector.astype(jnp.bfloat16)
        partial_rows = lax.dot_general(
            lax.all_gather(vector_half, "samp", axis=1, tiled=True),
            design_matrix,
            (((1,), (1,)), ((), ())),
            preferred_element_type=jnp.float32,
        )
        return lax.psum(partial_rows, "feat")

    def apply_columns(values):
        return lax.psum_scatter(
            lax.dot_general(
                design_matrix, values, (((0,), (1,)), ((), ())), preferred_element_type=jnp.float32
            ),
            "samp",
            scatter_dimension=0,
            tiled=True,
        ).T

    def precondition(residual):
        projected = jnp.dot(residual, sketch_full, precision=lax.Precision.HIGHEST)
        projected = lax.psum(projected, ("samp", "feat"))
        correction = lax.dot_general(
            ratios * projected,
            sketch_full,
            (((1,), (1,)), ((), ())),
            precision=lax.Precision.HIGHEST,
        )
        precond_res = residual + correction
        res_dot = lax.psum(jnp.sum(residual * precond_res, axis=1), ("samp", "feat"))
        return (precond_res, res_dot)

    logits = apply_rows(weights)
    probability = jax.nn.sigmoid(logits)
    hessian_diag = probability * (1.0 - probability)
    miss_rows = (probability - labels[None, :].astype(jnp.float32)).astype(jnp.bfloat16)
    gradient = apply_columns(miss_rows) + lambdas[:, None] * weights
    residual = -gradient
    precond_res, res_dot = precondition(residual)
    direction = precond_res
    update = jnp.zeros_like(residual)
    for iteration in range(ITERS):
        image_rows = apply_rows(direction)
        hess_dir = (
            apply_columns((hessian_diag * image_rows).astype(jnp.bfloat16))
            + lambdas[:, None] * direction
        )
        curvature = lax.psum(jnp.sum(direction * hess_dir, axis=1), ("samp", "feat"))
        step_size = res_dot / curvature
        update = update + step_size[:, None] * direction
        if iteration + 1 < ITERS:
            residual = residual - step_size[:, None] * hess_dir
            precond_res, new_dot = precondition(residual)
            direction = precond_res + (new_dot / res_dot)[:, None] * direction
            res_dot = new_dot
    return weights + update


def solution(mesh):
    return jax.shard_map(
        shards,
        mesh=mesh,
        in_specs=(
            P("samp", "feat"),
            P("samp"),
            P(None, ("feat", "samp")),
            P(),
            P(("feat", "samp"), None),
            P(),
        ),
        out_specs=P(None, ("feat", "samp")),
        check_vma=False,
    )
```

profile of v0, /device:TPU:10, one launch (start us, length us, event | category | flops | bytes accessed | tf_op | source)
XLA Modules:
  0.0 596.1 jit_solution(18189731865618623638)
XLA Ops:
  6.5 0.0 copy-start
  6.5 0.0 reduce-scatter.4.cloned.1.call-start
  6.5 0.7 convert_element_type.24
  7.3 0.8 convert_element_type.23
  8.1 33.0 %all_gather.9 = bf16[16,16384]{1,0:T(8,128)(2,1)S(1)} all-gather(bf16[16,1024]{1,0:T(8,128)(2,1)S(1)} %convert_element_type.23), channel_id=1, replica_groups=mesh['samp'=16,'feat'=2] {'samp'}, dimensions={1}, use_global_device_ids=true | all-gather | bytes 557056 | tf_op jit(solution)/shard_map/all_gather | solution.py:17
  41.1 3.4 fusion.22
  44.4 0.0 copy-start.3
  44.4 0.0 copy-start.2
  44.4 0.0 copy-start.1
  44.5 2.6 psum.63
  47.1 3.8 convolution_bitcast_fusion.2
  51.0 0.0 reduce-scatter.4.cloned.1.call-update
  51.0 0.0 reduce-scatter.6.cloned.1.call-start
  51.0 0.0 copy-done.3
  51.0 0.6 reduce_min.9
  51.6 0.0 copy-done.2
  51.6 0.6 broadcast_add_fusion
  52.3 73.3 %reduce-scatter.4.cloned.1.call-done = f32[1024,16]{0,1:T(8,128)} async-done(((f32[16384,16]{0,1:T(8,128)}), f32[1024,16]{0,1:T(8,128)}) %reduce-scatter.4.cloned.1.call-update) | async-done | bytes 65552 | tf_op jit(solution)/shard_map/reduce_scatter | solution.py:25
  125.6 0.0 copy-done.1
  125.6 0.9 fusion.2
  126.6 0.0 copy-done
  126.6 0.4 fusion.23
  127.0 50.1 %psum.64 = f32[16,384]{1,0:T(8,128)S(1)} all-reduce(f32[16,384]{1,0:T(8,128)S(1)} %fusion.23), channel_id=1, replica_groups=mesh['samp'=16,'feat'=2] {'samp','feat'}, use_global_device_ids=true, to_apply=%region_3.0 | all-reduce | flops 6144 | bytes 49152 | tf_op jit(solution)/shard_map/psum | solution.py:36
  177.1 0.7 fusion.21
  177.8 32.0 %all_gather.10 = bf16[16,16384]{1,0:T(8,128)(2,1)S(1)} all-gather(bf16[16,1024]{1,0:T(8,128)(2,1)S(1)} %get-tuple-element.9), channel_id=1, replica_groups=mesh['samp'=16,'feat'=2] {'samp'}, dimensions={1}, use_global_device_ids=true | all-gather | bytes 557056 | tf_op jit(solution)/shard_map/all_gather | solution.py:17
  209.8 3.4 fusion.24
  213.1 2.5 psum.66
  215.6 3.8 convolution_bitcast_fusion.1
  219.5 0.0 reduce-scatter.6.cloned.1.call-update
  219.5 0.0 reduce-scatter.8.cloned.1.call-start
  219.5 71.6 %reduce-scatter.6.cloned.1.call-done = f32[1024,16]{0,1:T(8,128)} async-done(((f32[16384,16]{0,1:T(8,128)}), f32[1024,16]{0,1:T(8,128)}) %reduce-scatter.6.cloned.1.call-update) | async-done | bytes 65552 | tf_op jit(solution)/shard_map/reduce_scatter | solution.py:25
  291.1 1.0 multiply_reduce_fusion.1
  292.1 49.7 %all-reduce = (f32[16]{0:T(128)S(1)}, f32[16]{0:T(128)S(1)}) all-reduce(f32[16]{0:T(128)S(1)} %get-tuple-element.6, f32[16]{0:T(128)S(1)} %get-tuple-element.5), channel_id=1, replica_groups=mesh['samp'=16,'feat'=2] {'samp','feat'}, use_global_device_ids=true, to_apply=%region_5.0 | all-reduce | flops 32 | bytes 256 | tf_op jit(solution)/shard_map/psum | solution.py:44
  341.9 0.9 multiply_subtract_fusion
  342.8 0.4 fusion.25
  343.2 38.3 %psum.68 = f32[16,384]{1,0:T(8,128)S(1)} all-reduce(f32[16,384]{1,0:T(8,128)S(1)} %fusion.25), channel_id=1, replica_groups=mesh['samp'=16,'feat'=2] {'samp','feat'}, use_global_device_ids=true, to_apply=%region_10.0 | all-reduce | flops 6144 | bytes 49152 | tf_op jit(solution)/shard_map/psum | solution.py:36
  381.5 0.8 multiply_reduce_fusion
  382.3 41.9 %psum.69 = f32[16]{0:T(128)S(1)} all-reduce(f32[16]{0:T(128)S(1)} %get-tuple-element.11), channel_id=1, replica_groups=mesh['samp'=16,'feat'=2] {'samp','feat'}, use_global_device_ids=true, to_apply=%region_12.0 | all-reduce | flops 16 | bytes 128 | tf_op jit(solution)/shard_map/psum | solution.py:44
  424.2 0.1 fusion.20
  424.3 31.8 %all_gather.11 = bf16[16,16384]{1,0:T(8,128)(2,1)S(1)} all-gather(bf16[16,1024]{1,0:T(8,128)(2,1)S(1)} %fusion.20), channel_id=1, replica_groups=mesh['samp'=16,'feat'=2] {'samp'}, dimensions={1}, use_global_device_ids=true | all-gather | bytes 557056 | tf_op jit(solution)/shard_map/all_gather | solution.py:17
  456.1 3.4 fusion.26
  459.5 2.5 psum.70
  462.0 3.9 convolution_bitcast_fusion
  465.8 0.0 reduce-scatter.8.cloned.1.call-update
  465.8 72.2 %reduce-scatter.8.cloned.1.call-done = f32[1024,16]{0,1:T(8,128)} async-done(((f32[16384,16]{0,1:T(8,128)}), f32[1024,16]{0,1:T(8,128)}) %reduce-scatter.8.cloned.1.call-update) | async-done | bytes 65552 | tf_op jit(solution)/shard_map/reduce_scatter | solution.py:25
  538.1 1.0 fusion.1
  539.1 49.8 %psum.71 = f32[16]{0:T(128)S(1)} all-reduce(f32[16]{0:T(128)S(1)} %fusion.1), channel_id=1, replica_groups=mesh['samp'=16,'feat'=2] {'samp','feat'}, use_global_device_ids=true, to_apply=%region_16.0 | all-reduce | flops 16 | bytes 128 | tf_op jit(solution)/shard_map/psum | solution.py:62
  588.9 0.7 add_add_fusion
  (3 shorter events, 0.0 us)
Async XLA Ops:
  6.5 120.0 %copy-start = (bf16[1024,384]{1,0:T(8,128)(2,1)S(1)}, bf16[1024,384]{1,0:T(8,128)(2,1)}, u32[]{:S(2)}) copy-start(bf16[1024,384]{1,0:T(8,128)(2,1)} %param.10) | copy-start | bytes 2359300
  6.5 119.1 %reduce-scatter.4.cloned.1.call-start = ((), (), s32[]{:S(2)}) async-start(), calls=%async_computation.3 | async-start | bytes 1114112 | tf_op jit(solution)/shard_map/reduce_scatter | solution.py:25
  44.4 6.6 %copy-start.3 = (f32[384]{0:T(512)S(1)}, f32[384]{0:T(512)}, u32[]{:S(2)}) copy-start(f32[384]{0:T(512)} %param.11) | copy-start | bytes 4612
  44.4 7.2 %copy-start.2 = (f32[16]{0:T(128)S(1)}, f32[16]{0:T(128)}, u32[]{:S(2)}) copy-start(f32[16]{0:T(128)} %param.9) | copy-start | bytes 196
  44.4 81.2 %copy-start.1 = (f32[16,1024]{1,0:T(8,128)S(1)}, f32[16,1024]{1,0:T(8,128)}, u32[]{:S(2)}) copy-start(f32[16,1024]{1,0:T(8,128)} %param.8) | copy-start | bytes 196612
  51.0 240.1 %reduce-scatter.6.cloned.1.call-start = ((), (), s32[]{:S(2)}) async-start(), calls=%async_computation.4 | async-start | bytes 1114112 | tf_op jit(solution)/shard_map/reduce_scatter | solution.py:25
  219.5 318.6 %reduce-scatter.8.cloned.1.call-start = ((), (), s32[]{:S(2)}) async-start(), calls=%async_computation.5 | async-start | bytes 1114112 | tf_op jit(solution)/shard_map/reduce_scatter | solution.py:25
Sparse Core Ops, SparseCore 0:
  51.1 74.4 reduce-scatter.3
  219.6 71.4 reduce-scatter.5
  466.0 72.0 reduce-scatter.7
where the time goes:
time: 597 us; the launch traced here: 596 us
  blocking collectives  334 us (56%)
  waiting for transfers between devices  217 us (36%)
  matrix products  24.1 us (4%)
  between operations  13.2 us (2%)
  other arithmetic  7.54 us (1%)
    reduce_scatter x3, waiting for transfers between devices, apply_columns(): lax.psum_scatter(lax.dot_general(design_matrix, values, (((0,), (1,)), ((...  217 us
    all_gather x3, blocking collectives, apply_rows(): lax.all_gather(vector_half, 'samp', axis=1, tiled=True)  96.7 us
    psum x2, blocking collectives, precondition(): lax.psum(jnp.sum(residual * precond_res, axis=1), ('samp', 'feat'))  91.6 us
    psum x2, blocking collectives, precondition(): projected = lax.psum(projected, ('samp', 'feat'))  88.3 us
    psum x1, blocking collectives, shards(): lax.psum(jnp.sum(direction * hess_dir, axis=1), ('samp', 'feat'))  49.8 us
  transfers between devices with their start and end apart: 3, of which 3 were waited for; matrix products, arithmetic and copies ran while one was open for 0% of the time, Pallas kernels for 0%

commit v1 on v0

--- a/solution.py
+++ b/solution.py
@@ -4,6 +4,10 @@
 from jax.sharding import PartitionSpec as P
 
 ITERS = 2
+
+
+def point_skins(slab_in, peer_axis):
+    return jnp.concatenate(lax.all_gather(slab_in, peer_axis), axis=1)
 
 
 def shards(design_matrix, labels, weights, lambdas, sketch, sketch_values):
@@ -14,7 +18,7 @@
     def apply_rows(vector):
         vector_half = vector.astype(jnp.bfloat16)
         partial_rows = lax.dot_general(
-            lax.all_gather(vector_half, "samp", axis=1, tiled=True),
+            point_skins(vector_half, "samp"),
             design_matrix,
             (((1,), (1,)), ((), ())),
             preferred_element_type=jnp.float32,

time: 597 us -> 597 us (level)
  no operation moved by 1% of the time
where the time goes in v1:
time: 597 us; the launch traced here: 596 us
  blocking collectives  334 us (56%)
  waiting for transfers between devices  217 us (36%)
  matrix products  24.1 us (4%)
  between operations  13.2 us (2%)
  other arithmetic  7.54 us (1%)
    reduce_scatter x3, waiting for transfers between devices, apply_columns(): lax.psum_scatter(lax.dot_general(design_matrix, values, (((0,), (1,)), ((...  217 us
    all_gather x3, blocking collectives, point_skins(): return jnp.concatenate(lax.all_gather(slab_in, peer_axis), axis=1)  96.7 us
    psum x2, blocking collectives, precondition(): lax.psum(jnp.sum(residual * precond_res, axis=1), ('samp', 'feat'))  91.6 us
    psum x2, blocking collectives, precondition(): projected = lax.psum(projected, ('samp', 'feat'))  88.3 us
    psum x1, blocking collectives, shards(): lax.psum(jnp.sum(direction * hess_dir, axis=1), ('samp', 'feat'))  49.8 us
  transfers between devices with their start and end apart: 3, of which 3 were waited for; matrix products, arithmetic and copies ran while one was open for 0% of the time, Pallas kernels for 0%

profile of v1, /device:TPU:10, one launch (start us, length us, event | category | flops | bytes accessed | tf_op | source)
XLA Modules:
  0.0 596.2 jit_solution(17795729915163834470)
XLA Ops:
  6.5 0.0 copy-start
  6.5 0.0 reduce-scatter.4.cloned.1.call-start
  6.5 0.7 convert_element_type.24
  7.3 0.8 convert_element_type.23
  8.1 33.0 %all-gather = bf16[256,1024]{1,0:T(8,128)(2,1)S(1)} all-gather(bf16[16,1024]{1,0:T(8,128)(2,1)S(1)} %convert_element_type.23), channel_id=2, replica_groups=mesh['samp'=16,'feat'=2] {'samp'}, dimensions={0}, use_global_device_ids=true | all-gather | bytes 557056 | tf_op jit(solution)/shard_map/all_gather | solution.py:10
  41.1 3.4 fusion.22
  44.5 0.0 copy-start.3
  44.5 0.0 copy-start.2
  44.5 0.0 copy-start.1
  44.5 2.6 psum.63
  47.1 3.8 convolution_bitcast_fusion.2
  51.0 0.0 reduce-scatter.4.cloned.1.call-update
  51.0 0.0 reduce-scatter.6.cloned.1.call-start
  51.1 0.0 copy-done.3
  51.1 0.6 reduce_min.9
  51.7 0.0 copy-done.2
  51.7 0.6 broadcast_add_fusion
  52.3 73.3 %reduce-scatter.4.cloned.1.call-done = f32[1024,16]{0,1:T(8,128)} async-done(((f32[16384,16]{0,1:T(8,128)}), f32[1024,16]{0,1:T(8,128)}) %reduce-scatter.4.cloned.1.call-update) | async-done | bytes 65552 | tf_op jit(solution)/shard_map/reduce_scatter | solution.py:29
  125.7 0.0 copy-done.1
  125.7 0.9 fusion.2
  126.6 0.0 copy-done
  126.6 0.4 fusion.23
  127.0 50.1 %psum.64 = f32[16,384]{1,0:T(8,128)S(1)} all-reduce(f32[16,384]{1,0:T(8,128)S(1)} %fusion.23), channel_id=1, replica_groups=mesh['samp'=16,'feat'=2] {'samp','feat'}, use_global_device_ids=true, to_apply=%region_3.0 | all-reduce | flops 6144 | bytes 49152 | tf_op jit(solution)/shard_map/psum | solution.py:40
  177.1 0.7 fusion.21
  177.8 32.0 %all-gather.1 = bf16[256,1024]{1,0:T(8,128)(2,1)S(1)} all-gather(bf16[16,1024]{1,0:T(8,128)(2,1)S(1)} %get-tuple-element.9), channel_id=3, replica_groups=mesh['samp'=16,'feat'=2] {'samp'}, dimensions={0}, use_global_device_ids=true | all-gather | bytes 557056 | tf_op jit(solution)/shard_map/all_gather | solution.py:10
  209.9 3.4 fusion.24
  213.2 2.5 psum.66
  215.7 3.8 convolution_bitcast_fusion.1
  219.6 0.0 reduce-scatter.6.cloned.1.call-update
  219.6 0.0 reduce-scatter.8.cloned.1.call-start
  219.6 71.6 %reduce-scatter.6.cloned.1.call-done = f32[1024,16]{0,1:T(8,128)} async-done(((f32[16384,16]{0,1:T(8,128)}), f32[1024,16]{0,1:T(8,128)}) %reduce-scatter.6.cloned.1.call-update) | async-done | bytes 65552 | tf_op jit(solution)/shard_map/reduce_scatter | solution.py:29
  291.2 1.0 multiply_reduce_fusion.1
  292.2 49.7 %all-reduce = (f32[16]{0:T(128)S(1)}, f32[16]{0:T(128)S(1)}) all-reduce(f32[16]{0:T(128)S(1)} %get-tuple-element.6, f32[16]{0:T(128)S(1)} %get-tuple-element.5), channel_id=1, replica_groups=mesh['samp'=16,'feat'=2] {'samp','feat'}, use_global_device_ids=true, to_apply=%region_5.0 | all-reduce | flops 32 | bytes 256 | tf_op jit(solution)/shard_map/psum | solution.py:48
  342.0 0.9 multiply_subtract_fusion
  342.9 0.4 fusion.25
  343.3 38.3 %psum.68 = f32[16,384]{1,0:T(8,128)S(1)} all-reduce(f32[16,384]{1,0:T(8,128)S(1)} %fusion.25), channel_id=1, replica_groups=mesh['samp'=16,'feat'=2] {'samp','feat'}, use_global_device_ids=true, to_apply=%region_10.0 | all-reduce | flops 6144 | bytes 49152 | tf_op jit(solution)/shard_map/psum | solution.py:40
  381.6 0.8 multiply_reduce_fusion
  382.4 41.9 %psum.69 = f32[16]{0:T(128)S(1)} all-reduce(f32[16]{0:T(128)S(1)} %get-tuple-element.11), channel_id=1, replica_groups=mesh['samp'=16,'feat'=2] {'samp','feat'}, use_global_device_ids=true, to_apply=%region_12.0 | all-reduce | flops 16 | bytes 128 | tf_op jit(solution)/shard_map/psum | solution.py:48
  424.3 0.1 fusion.20
  424.4 31.8 %all-gather.2 = bf16[256,1024]{1,0:T(8,128)(2,1)S(1)} all-gather(bf16[16,1024]{1,0:T(8,128)(2,1)S(1)} %fusion.20), channel_id=4, replica_groups=mesh['samp'=16,'feat'=2] {'samp'}, dimensions={0}, use_global_device_ids=true | all-gather | bytes 557056 | tf_op jit(solution)/shard_map/all_gather | solution.py:10
  456.2 3.4 fusion.26
  459.6 2.5 psum.70
  462.1 3.9 convolution_bitcast_fusion
  466.0 0.0 reduce-scatter.8.cloned.1.call-update
  466.0 72.2 %reduce-scatter.8.cloned.1.call-done = f32[1024,16]{0,1:T(8,128)} async-done(((f32[16384,16]{0,1:T(8,128)}), f32[1024,16]{0,1:T(8,128)}) %reduce-scatter.8.cloned.1.call-update) | async-done | bytes 65552 | tf_op jit(solution)/shard_map/reduce_scatter | solution.py:29
  538.2 1.0 fusion.1
  539.2 49.8 %psum.71 = f32[16]{0:T(128)S(1)} all-reduce(f32[16]{0:T(128)S(1)} %fusion.1), channel_id=1, replica_groups=mesh['samp'=16,'feat'=2] {'samp','feat'}, use_global_device_ids=true, to_apply=%region_16.0 | all-reduce | flops 16 | bytes 128 | tf_op jit(solution)/shard_map/psum | solution.py:66
  589.0 0.7 add_add_fusion
  (6 shorter events, 0.1 us)
Async XLA Ops:
  6.5 120.1 %copy-start = (bf16[1024,384]{1,0:T(8,128)(2,1)S(1)}, bf16[1024,384]{1,0:T(8,128)(2,1)}, u32[]{:S(2)}) copy-start(bf16[1024,384]{1,0:T(8,128)(2,1)} %param.10) | copy-start | bytes 2359300
  6.5 119.1 %reduce-scatter.4.cloned.1.call-start = ((), (), s32[]{:S(2)}) async-start(), calls=%async_computation.3 | async-start | bytes 1114112 | tf_op jit(solution)/shard_map/reduce_scatter | solution.py:29
  44.5 6.6 %copy-start.3 = (f32[384]{0:T(512)S(1)}, f32[384]{0:T(512)}, u32[]{:S(2)}) copy-start(f32[384]{0:T(512)} %param.11) | copy-start | bytes 4612
  44.5 7.2 %copy-start.2 = (f32[16]{0:T(128)S(1)}, f32[16]{0:T(128)}, u32[]{:S(2)}) copy-start(f32[16]{0:T(128)} %param.9) | copy-start | bytes 196
  44.5 81.2 %copy-start.1 = (f32[16,1024]{1,0:T(8,128)S(1)}, f32[16,1024]{1,0:T(8,128)}, u32[]{:S(2)}) copy-start(f32[16,1024]{1,0:T(8,128)} %param.8) | copy-start | bytes 196612
  51.0 240.2 %reduce-scatter.6.cloned.1.call-start = ((), (), s32[]{:S(2)}) async-start(), calls=%async_computation.4 | async-start | bytes 1114112 | tf_op jit(solution)/shard_map/reduce_scatter | solution.py:29
  219.6 318.6 %reduce-scatter.8.cloned.1.call-start = ((), (), s32[]{:S(2)}) async-start(), calls=%async_computation.5 | async-start | bytes 1114112 | tf_op jit(solution)/shard_map/reduce_scatter | solution.py:29
Sparse Core Ops, SparseCore 0:
  51.1 74.4 reduce-scatter.3
  219.7 71.4 reduce-scatter.5
  466.1 72.0 reduce-scatter.7
